TPU v7x, 64 devices: a 2x2x8 block of a 4x4x8 slice. The times are simulated.
64 devices in a mesh: dp: 4 (over x, y), tp: 16 (over z, core).
Axes of the slice: x: 2, y: 2, z: 8, core: 2. Of those that a mesh axis runs over, the one named last changes fastest.
The devices are a block of a 4x4x8 slice.
Arguments:
- x_in: bfloat16 [4096, 8192], P('dp'), parts along dimension 0
- g_norm: bfloat16 [8192], replicated
- w_q: bfloat16 [8192, 8192], P(None, 'tp')
- w_k: bfloat16 [8192, 1024], replicated
- w_v: bfloat16 [8192, 1024], replicated
- w_o: bfloat16 [8192, 8192], P('tp')
- w_gate: bfloat16 [8192, 22016], P(None, 'tp')
- w_up: bfloat16 [8192, 22016], P(None, 'tp')
- w_down: bfloat16 [22016, 8192], P('tp')
Outputs:
- output 1: bfloat16 [4096, 8192], P('dp'), parts along dimension 0
- output 2: bfloat16 [4096, 16, 128], P('dp', 'tp'), parts along dimension 0
- output 3: bfloat16 [4096, 16, 128], P('dp', 'tp'), parts along dimension 0
There are 4 independent parts. A program takes and returns all parts, laid end to end along the dimension named above; an argument that names none is the same for every part.
All inputs are finite; a program needn't handle non-finite values.
Results may differ from a plain program's by a relative error of at most 0.0157075.
Values are sent between devices in bfloat16 or wider.
A program may use at most 768 MiB of HBM per device.

v0:
```python
import math
import jax
import jax.numpy as jnp
from jax import lax
from jax.sharding import PartitionSpec as P

HEAD_DIM = 128
ROPE_BASE = 500000.0
NORM_EPS = 1e-5


def rope_tables(positions):
    inv_freq = ROPE_BASE ** (-jnp.arange(0, HEAD_DIM, 2, dtype=jnp.float32) / HEAD_DIM)
    angles = positions.astype(jnp.float32)[:, None] * inv_freq[None, :]
    return jnp.cos(angles), jnp.sin(angles)


def apply_rope(projected, cos_tab, sin_tab):
    half_dim = HEAD_DIM // 2
    lower_half = projected[..., :half_dim]
    upper_half = projected[..., half_dim:]
    cos_b = cos_tab[:, None, :]
    sin_b = sin_tab[:, None, :]
    return jnp.concatenate([lower_half * cos_b - upper_half * sin_b, upper_half * cos_b + lower_half * sin_b], axis=-1)


def rms_norm(x_rows, g_norm):
    x_f32 = x_rows.astype(jnp.float32)
    inv_rms = lax.rsqrt(jnp.mean(x_f32 * x_f32, axis=-1, keepdims=True) + NORM_EPS)
    return (x_f32 * inv_rms * g_norm.astype(jnp.float32)).astype(jnp.bfloat16)


def solution(mesh):
    tp_size = mesh.shape['tp']

    def local_layer(x_in, g_norm, w_q, w_k, w_v, w_o, w_gate, w_up, w_down):
        tokens, width = x_in.shape
        kv_heads = w_k.shape[1] // HEAD_DIM
        kv_local = max(kv_heads // tp_size, 1)
        q_local = w_q.shape[1] // HEAD_DIM
        group_size = q_local // kv_local
        q_block = min(128, tokens)
        score_scale = 1.0 / math.sqrt(HEAD_DIM)
        head_start = lax.axis_index('tp') * kv_heads // tp_size
        normed = rms_norm(x_in, g_norm)
        cos_tab, sin_tab = rope_tables(jnp.arange(tokens))
        w_k_mine = lax.dynamic_slice_in_dim(w_k, head_start * HEAD_DIM, kv_local * HEAD_DIM, axis=1)
        w_v_mine = lax.dynamic_slice_in_dim(w_v, head_start * HEAD_DIM, kv_local * HEAD_DIM, axis=1)
        k_proj = jnp.dot(normed, w_k_mine, preferred_element_type=jnp.float32).reshape(tokens, kv_local, HEAD_DIM)
        k_rot = apply_rope(k_proj, cos_tab, sin_tab).astype(jnp.bfloat16)
        v_proj = jnp.dot(normed, w_v_mine, preferred_element_type=jnp.float32).astype(jnp.bfloat16).reshape(tokens, kv_local, HEAD_DIM)
        key_pos = jnp.arange(tokens)

        def row_block(block_idx):
            row_start = block_idx * q_block
            normed_blk = lax.dynamic_slice_in_dim(normed, row_start, q_block, axis=0)
            cos_blk = lax.dynamic_slice_in_dim(cos_tab, row_start, q_block, axis=0)
            sin_blk = lax.dynamic_slice_in_dim(sin_tab, row_start, q_block, axis=0)
            q_proj = jnp.dot(normed_blk, w_q, preferred_element_type=jnp.float32).reshape(q_block, q_local, HEAD_DIM)
            q_rot = apply_rope(q_proj, cos_blk, sin_blk).astype(jnp.bfloat16).reshape(q_block, kv_local, group_size, HEAD_DIM)
            scores = jnp.einsum('qgrd,kgd->grqk', q_rot, k_rot, preferred_element_type=jnp.float32) * score_scale
            query_pos = row_start + jnp.arange(q_block)
            scores = jnp.where(key_pos[None, :] <= query_pos[:, None], scores, -1e30)
            probs_bf = jax.nn.softmax(scores, axis=-1).astype(jnp.bfloat16)
            attn_out = jnp.einsum('grqk,kgd->qgrd', probs_bf, v_proj, preferred_element_type=jnp.float32).astype(jnp.bfloat16).reshape(q_block, q_local * HEAD_DIM)
            gate_proj = jnp.dot(normed_blk, w_gate, preferred_element_type=jnp.float32)
            up_proj = jnp.dot(normed_blk, w_up, preferred_element_type=jnp.float32)
            hidden = (jax.nn.silu(gate_proj) * up_proj).astype(jnp.bfloat16)
            return (jnp.dot(attn_out, w_o, preferred_element_type=jnp.float32) + jnp.dot(hidden, w_down, preferred_element_type=jnp.float32)).astype(jnp.bfloat16)

        partial_sum = lax.map(row_block, jnp.arange(tokens // q_block)).reshape(tokens, width)
        reduced_sum = lax.psum(partial_sum, 'tp')
        y_out = (x_in.astype(jnp.float32) + reduced_sum.astype(jnp.float32)).astype(jnp.bfloat16)
        return y_out, k_rot, v_proj

    return jax.shard_map(local_layer, mesh=mesh, in_specs=(P('dp', None), P(None), P(None, 'tp'), P(None, None), P(None, None), P('tp', None), P(None, 'tp'), P(None, 'tp'), P('tp', None)), out_specs=(P('dp', None), P('dp', 'tp', None), P('dp', 'tp', None)), check_vma=False)
```

profile of v0, /device:TPU:21, one launch (start us, length us, event | category | flops | bytes accessed | tf_op | source)
XLA Modules:
  0.0 708.1 jit_solution(938412544821973008)
XLA Ops:
  7.3 0.7 convert_element_type.70
  8.0 7.2 %fusion.32 = f32[1024]{0:T(1024)S(1)} fusion(bf16[1024,8192]{1,0:T(8,128)(2,1)} %param.11), kind=kLoop, calls=%fused_computation.44 | loop fusion | flops 25164800 | bytes 16781312 | tf_op jit(solution)/shard_map/reduce_sum | solution.py:29
  15.2 15.2 %fusion.34 = bf16[1024,8192]{1,0:T(8,128)(2,1)} fusion(bf16[1024,8192]{1,0:T(8,128)(2,1)} %param.11, f32[8192]{0:T(1024)S(1)} %convert_element_type.70, f32[1024]{0:T(1024)S(1)} %add_rsqrt_fusion), kind=kLoop, calls=%fused_computation.46 | loop fusion | flops 33554432 | bytes 33591296 | tf_op jit(solution)/shard_map/convert_element_type | solution.py:30
  30.4 1.9 multiply_sine_fusion
  32.3 12.0 %fusion.40 = f32[1024,1,128]{0,2,1:T(8,128)S(1)} fusion(bf16[1024,8192]{1,0:T(8,128)(2,1)} %fusion.34, bf16[8192,1024]{1,0:T(8,128)(2,1)} %param.14, s32[]{:T(128)S(6)} %select_n.19), kind=kOutput, calls=%fused_computation.52 | convolution fusion | flops 2147483648 | bytes 19398660 | tf_op jit(solution)/shard_map/dot_general | solution.py:49
  44.4 1.2 fusion.54
  45.7 10.8 %fusion.46 = bf16[1024,1,128]{2,0,1:T(8,128)(2,1)S(1)} fusion(bf16[1024,8192]{1,0:T(8,128)(2,1)} %fusion.34, bf16[8192,1024]{1,0:T(8,128)(2,1)} %param.15, s32[]{:T(128)S(6)} %select_n.19), kind=kOutput, calls=%fused_computation.54 | convolution fusion | flops 2147614720 | bytes 19136516 | tf_op jit(solution)/shard_map/dot_general | solution.py:51
  57.3 428.4 %while.11 = (s32[]{:T(128)}, bf16[8,128,8192]{2,1,0:T(8,128)(2,1)}, s32[8]{0:T(128)S(1)}, bf16[1024,8192]{1,0:T(8,128)(2,1)}, bf16[8192,512]{1,0:T(8,128)(2,1)},...) while((s32[]{:T(128)}, bf16[8,128,8192]{2,1,0:T(8,128)(2,1)}, ...), condition=%wide.region_4.5_spmd.clone, body=%wide.region_1.4_spmd.clone.sunk | while | flops 11081031680 | bytes 111980256 | solution.py:71
  58.7 5.3 fusion.100
  65.7 0.7 convolution_convert_fusion.2
  66.4 11.1 %fusion.98 = f32[128,1376]{0,1:T(8,128)S(1)} fusion(bf16[8192,1376]{0,1:T(8,128)(2,1)} %get-tuple-element.297, bf16[1024,8192]{1,0:T(8,128)(2,1)} %get-tuple-element.290, s32[]{:T(128)S(6)} %select_n.24), kind=kOutput, calls=%fused_computation.13.clone.1 | convolution fusion | flops 2885681152 | bytes 25346052 | tf_op jit(solution)/shard_map/while/body/eval_jaxpr/dot_general | solution.py:66
  77.5 26.0 %fusion.99 = f32[128,8192]{1,0:T(8,128)} fusion(bf16[1376,8192]{1,0:T(8,128)(2,1)} %get-tuple-element.299, bf16[8192,1376]{0,1:T(8,128)(2,1)} %get-tuple-element.298, bf16[1024,8192]{1,0:T(8,128)(2,1)} %get-tuple-element.290, s32[]{:T(128)S(6)} %select_n.24, f32[128,1376]{0,1:T(8,128)S(1)} %fusion.98), kind=kOutput, calls=%fused_computation.7.clone.1 | convolution fusion | flops 5772419072 | bytes 52084740 | tf_op jit(solution)/shard_map/while/body/eval_jaxpr/dot_general | solution.py:69
  103.5 7.3 %fusion.104 = bf16[8,128,8192]{2,1,0:T(8,128)(2,1)} fusion(bf16[8,128,8192]{2,1,0:T(8,128)(2,1)} %get-tuple-element.271, s32[]{:T(128)} %get-tuple-element.270, f32[128,8192]{1,0:T(8,128)} %fusion.99, bf16[128,512]{0,1:T(8,128)(2,1)S(1)} %bitcast.69, bf16[512,8192]{1,0:T(8,128)(2,1)} %get-tuple-element.296), kind=kOutput, calls=%fused_computation.4.clone.1 | convolution fusion | flops 1075838976 | bytes 14811648 | tf_op jit(solution)/shard_map/while/body/eval_jaxpr/dot_general | solution.py:69
  112.2 5.3 fusion.100
  119.2 0.7 convolution_convert_fusion.2
  119.9 11.1 %fusion.98 = f32[128,1376]{0,1:T(8,128)S(1)} fusion(bf16[8192,1376]{0,1:T(8,128)(2,1)} %get-tuple-element.297, bf16[1024,8192]{1,0:T(8,128)(2,1)} %get-tuple-element.290, s32[]{:T(128)S(6)} %select_n.24), kind=kOutput, calls=%fused_computation.13.clone.1 | convolution fusion | flops 2885681152 | bytes 25346052 | tf_op jit(solution)/shard_map/while/body/eval_jaxpr/dot_general | solution.py:66
  131.1 26.1 %fusion.99 = f32[128,8192]{1,0:T(8,128)} fusion(bf16[1376,8192]{1,0:T(8,128)(2,1)} %get-tuple-element.299, bf16[8192,1376]{0,1:T(8,128)(2,1)} %get-tuple-element.298, bf16[1024,8192]{1,0:T(8,128)(2,1)} %get-tuple-element.290, s32[]{:T(128)S(6)} %select_n.24, f32[128,1376]{0,1:T(8,128)S(1)} %fusion.98), kind=kOutput, calls=%fused_computation.7.clone.1 | convolution fusion | flops 5772419072 | bytes 52084740 | tf_op jit(solution)/shard_map/while/body/eval_jaxpr/dot_general | solution.py:69
  157.2 7.3 %fusion.104 = bf16[8,128,8192]{2,1,0:T(8,128)(2,1)} fusion(bf16[8,128,8192]{2,1,0:T(8,128)(2,1)} %get-tuple-element.271, s32[]{:T(128)} %get-tuple-element.270, f32[128,8192]{1,0:T(8,128)} %fusion.99, bf16[128,512]{0,1:T(8,128)(2,1)S(1)} %bitcast.69, bf16[512,8192]{1,0:T(8,128)(2,1)} %get-tuple-element.296), kind=kOutput, calls=%fused_computation.4.clone.1 | convolution fusion | flops 1075838976 | bytes 14811648 | tf_op jit(solution)/shard_map/while/body/eval_jaxpr/dot_general | solution.py:69
  165.8 5.3 fusion.100
  172.9 0.7 convolution_convert_fusion.2
  173.5 11.1 %fusion.98 = f32[128,1376]{0,1:T(8,128)S(1)} fusion(bf16[8192,1376]{0,1:T(8,128)(2,1)} %get-tuple-element.297, bf16[1024,8192]{1,0:T(8,128)(2,1)} %get-tuple-element.290, s32[]{:T(128)S(6)} %select_n.24), kind=kOutput, calls=%fused_computation.13.clone.1 | convolution fusion | flops 2885681152 | bytes 25346052 | tf_op jit(solution)/shard_map/while/body/eval_jaxpr/dot_general | solution.py:66
  184.7 26.1 %fusion.99 = f32[128,8192]{1,0:T(8,128)} fusion(bf16[1376,8192]{1,0:T(8,128)(2,1)} %get-tuple-element.299, bf16[8192,1376]{0,1:T(8,128)(2,1)} %get-tuple-element.298, bf16[1024,8192]{1,0:T(8,128)(2,1)} %get-tuple-element.290, s32[]{:T(128)S(6)} %select_n.24, f32[128,1376]{0,1:T(8,128)S(1)} %fusion.98), kind=kOutput, calls=%fused_computation.7.clone.1 | convolution fusion | flops 5772419072 | bytes 52084740 | tf_op jit(solution)/shard_map/while/body/eval_jaxpr/dot_general | solution.py:69
  210.7 7.3 %fusion.104 = bf16[8,128,8192]{2,1,0:T(8,128)(2,1)} fusion(bf16[8,128,8192]{2,1,0:T(8,128)(2,1)} %get-tuple-element.271, s32[]{:T(128)} %get-tuple-element.270, f32[128,8192]{1,0:T(8,128)} %fusion.99, bf16[128,512]{0,1:T(8,128)(2,1)S(1)} %bitcast.69, bf16[512,8192]{1,0:T(8,128)(2,1)} %get-tuple-element.296), kind=kOutput, calls=%fused_computation.4.clone.1 | convolution fusion | flops 1075838976 | bytes 14811648 | tf_op jit(solution)/shard_map/while/body/eval_jaxpr/dot_general | solution.py:69
  219.4 5.3 fusion.100
  227.1 11.1 %fusion.98 = f32[128,1376]{0,1:T(8,128)S(1)} fusion(bf16[8192,1376]{0,1:T(8,128)(2,1)} %get-tuple-element.297, bf16[1024,8192]{1,0:T(8,128)(2,1)} %get-tuple-element.290, s32[]{:T(128)S(6)} %select_n.24), kind=kOutput, calls=%fused_computation.13.clone.1 | convolution fusion | flops 2885681152 | bytes 25346052 | tf_op jit(solution)/shard_map/while/body/eval_jaxpr/dot_general | solution.py:66
  238.2 26.0 %fusion.99 = f32[128,8192]{1,0:T(8,128)} fusion(bf16[1376,8192]{1,0:T(8,128)(2,1)} %get-tuple-element.299, bf16[8192,1376]{0,1:T(8,128)(2,1)} %get-tuple-element.298, bf16[1024,8192]{1,0:T(8,128)(2,1)} %get-tuple-element.290, s32[]{:T(128)S(6)} %select_n.24, f32[128,1376]{0,1:T(8,128)S(1)} %fusion.98), kind=kOutput, calls=%fused_computation.7.clone.1 | convolution fusion | flops 5772419072 | bytes 52084740 | tf_op jit(solution)/shard_map/while/body/eval_jaxpr/dot_general | solution.py:69
  264.2 7.3 %fusion.104 = bf16[8,128,8192]{2,1,0:T(8,128)(2,1)} fusion(bf16[8,128,8192]{2,1,0:T(8,128)(2,1)} %get-tuple-element.271, s32[]{:T(128)} %get-tuple-element.270, f32[128,8192]{1,0:T(8,128)} %fusion.99, bf16[128,512]{0,1:T(8,128)(2,1)S(1)} %bitcast.69, bf16[512,8192]{1,0:T(8,128)(2,1)} %get-tuple-element.296), kind=kOutput, calls=%fused_computation.4.clone.1 | convolution fusion | flops 1075838976 | bytes 14811648 | tf_op jit(solution)/shard_map/while/body/eval_jaxpr/dot_general | solution.py:69
  272.9 5.3 fusion.100
  279.9 0.7 convolution_convert_fusion.2
  280.6 11.1 %fusion.98 = f32[128,1376]{0,1:T(8,128)S(1)} fusion(bf16[8192,1376]{0,1:T(8,128)(2,1)} %get-tuple-element.297, bf16[1024,8192]{1,0:T(8,128)(2,1)} %get-tuple-element.290, s32[]{:T(128)S(6)} %select_n.24), kind=kOutput, calls=%fused_computation.13.clone.1 | convolution fusion | flops 2885681152 | bytes 25346052 | tf_op jit(solution)/shard_map/while/body/eval_jaxpr/dot_general | solution.py:66
  291.7 26.1 %fusion.99 = f32[128,8192]{1,0:T(8,128)} fusion(bf16[1376,8192]{1,0:T(8,128)(2,1)} %get-tuple-element.299, bf16[8192,1376]{0,1:T(8,128)(2,1)} %get-tuple-element.298, bf16[1024,8192]{1,0:T(8,128)(2,1)} %get-tuple-element.290, s32[]{:T(128)S(6)} %select_n.24, f32[128,1376]{0,1:T(8,128)S(1)} %fusion.98), kind=kOutput, calls=%fused_computation.7.clone.1 | convolution fusion | flops 5772419072 | bytes 52084740 | tf_op jit(solution)/shard_map/while/body/eval_jaxpr/dot_general | solution.py:69
  317.8 7.3 %fusion.104 = bf16[8,128,8192]{2,1,0:T(8,128)(2,1)} fusion(bf16[8,128,8192]{2,1,0:T(8,128)(2,1)} %get-tuple-element.271, s32[]{:T(128)} %get-tuple-element.270, f32[128,8192]{1,0:T(8,128)} %fusion.99, bf16[128,512]{0,1:T(8,128)(2,1)S(1)} %bitcast.69, bf16[512,8192]{1,0:T(8,128)(2,1)} %get-tuple-element.296), kind=kOutput, calls=%fused_computation.4.clone.1 | convolution fusion | flops 1075838976 | bytes 14811648 | tf_op jit(solution)/shard_map/while/body/eval_jaxpr/dot_general | solution.py:69
  326.5 5.3 fusion.100
  334.2 11.1 %fusion.98 = f32[128,1376]{0,1:T(8,128)S(1)} fusion(bf16[8192,1376]{0,1:T(8,128)(2,1)} %get-tuple-element.297, bf16[1024,8192]{1,0:T(8,128)(2,1)} %get-tuple-element.290, s32[]{:T(128)S(6)} %select_n.24), kind=kOutput, calls=%fused_computation.13.clone.1 | convolution fusion | flops 2885681152 | bytes 25346052 | tf_op jit(solution)/shard_map/while/body/eval_jaxpr/dot_general | solution.py:66
  345.3 26.0 %fusion.99 = f32[128,8192]{1,0:T(8,128)} fusion(bf16[1376,8192]{1,0:T(8,128)(2,1)} %get-tuple-element.299, bf16[8192,1376]{0,1:T(8,128)(2,1)} %get-tuple-element.298, bf16[1024,8192]{1,0:T(8,128)(2,1)} %get-tuple-element.290, s32[]{:T(128)S(6)} %select_n.24, f32[128,1376]{0,1:T(8,128)S(1)} %fusion.98), kind=kOutput, calls=%fused_computation.7.clone.1 | convolution fusion | flops 5772419072 | bytes 52084740 | tf_op jit(solution)/shard_map/while/body/eval_jaxpr/dot_general | solution.py:69
  371.3 7.3 %fusion.104 = bf16[8,128,8192]{2,1,0:T(8,128)(2,1)} fusion(bf16[8,128,8192]{2,1,0:T(8,128)(2,1)} %get-tuple-element.271, s32[]{:T(128)} %get-tuple-element.270, f32[128,8192]{1,0:T(8,128)} %fusion.99, bf16[128,512]{0,1:T(8,128)(2,1)S(1)} %bitcast.69, bf16[512,8192]{1,0:T(8,128)(2,1)} %get-tuple-element.296), kind=kOutput, calls=%fused_computation.4.clone.1 | convolution fusion | flops 1075838976 | bytes 14811648 | tf_op jit(solution)/shard_map/while/body/eval_jaxpr/dot_general | solution.py:69
  379.9 5.3 fusion.100
  387.0 0.7 convolution_convert_fusion.2
  387.7 11.1 %fusion.98 = f32[128,1376]{0,1:T(8,128)S(1)} fusion(bf16[8192,1376]{0,1:T(8,128)(2,1)} %get-tuple-element.297, bf16[1024,8192]{1,0:T(8,128)(2,1)} %get-tuple-element.290, s32[]{:T(128)S(6)} %select_n.24), kind=kOutput, calls=%fused_computation.13.clone.1 | convolution fusion | flops 2885681152 | bytes 25346052 | tf_op jit(solution)/shard_map/while/body/eval_jaxpr/dot_general | solution.py:66
  398.8 26.0 %fusion.99 = f32[128,8192]{1,0:T(8,128)} fusion(bf16[1376,8192]{1,0:T(8,128)(2,1)} %get-tuple-element.299, bf16[8192,1376]{0,1:T(8,128)(2,1)} %get-tuple-element.298, bf16[1024,8192]{1,0:T(8,128)(2,1)} %get-tuple-element.290, s32[]{:T(128)S(6)} %select_n.24, f32[128,1376]{0,1:T(8,128)S(1)} %fusion.98), kind=kOutput, calls=%fused_computation.7.clone.1 | convolution fusion | flops 5772419072 | bytes 52084740 | tf_op jit(solution)/shard_map/while/body/eval_jaxpr/dot_general | solution.py:69
  424.8 7.3 %fusion.104 = bf16[8,128,8192]{2,1,0:T(8,128)(2,1)} fusion(bf16[8,128,8192]{2,1,0:T(8,128)(2,1)} %get-tuple-element.271, s32[]{:T(128)} %get-tuple-element.270, f32[128,8192]{1,0:T(8,128)} %fusion.99, bf16[128,512]{0,1:T(8,128)(2,1)S(1)} %bitcast.69, bf16[512,8192]{1,0:T(8,128)(2,1)} %get-tuple-element.296), kind=kOutput, calls=%fused_computation.4.clone.1 | convolution fusion | flops 1075838976 | bytes 14811648 | tf_op jit(solution)/shard_map/while/body/eval_jaxpr/dot_general | solution.py:69
  433.5 5.3 fusion.100
  440.5 0.7 convolution_convert_fusion.2
  441.2 11.1 %fusion.98 = f32[128,1376]{0,1:T(8,128)S(1)} fusion(bf16[8192,1376]{0,1:T(8,128)(2,1)} %get-tuple-element.297, bf16[1024,8192]{1,0:T(8,128)(2,1)} %get-tuple-element.290, s32[]{:T(128)S(6)} %select_n.24), kind=kOutput, calls=%fused_computation.13.clone.1 | convolution fusion | flops 2885681152 | bytes 25346052 | tf_op jit(solution)/shard_map/while/body/eval_jaxpr/dot_general | solution.py:66
  452.3 26.1 %fusion.99 = f32[128,8192]{1,0:T(8,128)} fusion(bf16[1376,8192]{1,0:T(8,128)(2,1)} %get-tuple-element.299, bf16[8192,1376]{0,1:T(8,128)(2,1)} %get-tuple-element.298, bf16[1024,8192]{1,0:T(8,128)(2,1)} %get-tuple-element.290, s32[]{:T(128)S(6)} %select_n.24, f32[128,1376]{0,1:T(8,128)S(1)} %fusion.98), kind=kOutput, calls=%fused_computation.7.clone.1 | convolution fusion | flops 5772419072 | bytes 52084740 | tf_op jit(solution)/shard_map/while/body/eval_jaxpr/dot_general | solution.py:69
  478.4 7.3 %fusion.104 = bf16[8,128,8192]{2,1,0:T(8,128)(2,1)} fusion(bf16[8,128,8192]{2,1,0:T(8,128)(2,1)} %get-tuple-element.271, s32[]{:T(128)} %get-tuple-element.270, f32[128,8192]{1,0:T(8,128)} %fusion.99, bf16[128,512]{0,1:T(8,128)(2,1)S(1)} %bitcast.69, bf16[512,8192]{1,0:T(8,128)(2,1)} %get-tuple-element.296), kind=kOutput, calls=%fused_computation.4.clone.1 | convolution fusion | flops 1075838976 | bytes 14811648 | tf_op jit(solution)/shard_map/while/body/eval_jaxpr/dot_general | solution.py:69
  485.8 197.2 %all-reduce.2.cloned.1.call-done = bf16[1024,8192]{1,0:T(8,128)(2,1)} async-done(((bf16[1024,8192]{1,0:T(8,128)(2,1)}), bf16[1024,8192]{1,0:T(8,128)(2,1)}) %all-reduce.2.cloned.1.call-update) | async-done | bytes 16777232 | tf_op jit(solution)/shard_map/psum | solution.py:72
  683.0 18.2 %fusion.35 = bf16[1024,8192]{1,0:T(8,128)(2,1)} fusion(bf16[1024,8192]{1,0:T(8,128)(2,1)} %param.11, bf16[1024,8192]{1,0:T(8,128)(2,1)} %all-reduce.2.cloned.1.call-done), kind=kLoop, calls=%fused_computation.47 | loop fusion | flops 33554432 | bytes 50331648 | tf_op jit(solution)/shard_map/convert_element_type | solution.py:73
  (88 shorter events, 21.3 us)
Async XLA Ops:
  7.2 675.8 %all-reduce.2.cloned.1.call-start = ((), (), s32[]{:S(2)}) async-start(), calls=%async_computation | async-start | bytes 33554432 | tf_op jit(solution)/shard_map/psum | solution.py:72
  56.6 0.7 copy-start.1
  485.7 215.5 %copy-start = (bf16[1024,1,128]{2,0,1:T(8,128)(2,1)}, bf16[1024,1,128]{2,0,1:T(8,128)(2,1)S(1)}, u32[]{:S(2)}) copy-start(bf16[1024,1,128]{2,0,1:T(8,128)(2,1)S(1)} %get-tuple-element.308) | copy-start | bytes 786436
Sparse Core Ops, SparseCore 0:
  485.9 196.9 all-reduce.1
where the time goes:
time: 708 us
  matrix products  431 us (61%)
  waiting for transfers between devices  197 us (28%)
  other arithmetic  50.4 us (7%)
  between operations  14.2 us (2%)
  local copies, waits for them, and re-layouts  8.61 us (1%)
    dot_general x8, matrix products, row_block(): jnp.dot(hidden, w_down, preferred_element_type=jnp.float32)  208 us
    psum x1, waiting for transfers between devices, local_layer(): reduced_sum = lax.psum(partial_sum, 'tp')  197 us
    dot_general x8, matrix products, row_block(): gate_proj = jnp.dot(normed_blk, w_gate, preferred_element_type=jnp.float32)  89 us
    dot_general x8, matrix products, row_block(): jnp.dot(attn_out, w_o, preferred_element_type=jnp.float32)  58.4 us
    dot_general x8, matrix products, row_block(): jnp.dot(normed_blk, w_q, preferred_element_type=jnp.float32)  42.2 us
    convert_element_type x1, other arithmetic, local_layer(): (x_in.astype(jnp.float32) + reduced_sum.astype(jnp.float32)).astype(jnp.b...  18.2 us
    convert_element_type x2, other arithmetic, rms_norm(): return (x_f32 * inv_rms * g_norm.astype(jnp.float32)).astype(jnp.bfloat16)  15.9 us
  transfers between devices with their start and end apart: 1, of which 1 were waited for; matrix products, arithmetic and copies ran while one was open for 0% of the time, Pallas kernels for 0%

commit v1 on v0

v1 whole, which is shorter than its diff:
```python
import functools
import math
import jax
import jax.numpy as jnp
from jax import lax
from jax.experimental import pallas as pl
from jax.experimental.pallas import tpu as pltpu
from jax.sharding import PartitionSpec as P

HEAD_DIM = 128
ROPE_BASE = 500000.0
NORM_EPS = 1e-5

ROW_BLOCKS = 4
K_STEPS = 16
N_STEPS = 8
SUBS = 4
MESH = pl.DeviceIdType.MESH


def rope_tables(positions):
    inv_freq = ROPE_BASE ** (-jnp.arange(0, HEAD_DIM, 2, dtype=jnp.float32) / HEAD_DIM)
    angles = positions.astype(jnp.float32)[:, None] * inv_freq[None, :]
    return jnp.cos(angles), jnp.sin(angles)


def round_up(n, m):
    return (n + m - 1) // m * m


def layer_kernel(cfg, x_hbm, g_ref, cos_ref, sin_ref, wq_hbm, wk_hbm, wv_hbm, wo_hbm, wg_hbm, wu_hbm, wd_hbm,
                 y_hbm, k_hbm, v_hbm,
                 xbuf, a_buf, wgu, wqkv, wo_buf, wd_buf, acc_gu, acc_qkv, m_buf, o_buf, q_buf, k_buf, v_buf,
                 pbuf, precv, rsbuf, ybuf, xown,
                 x_sem, wk_sem, wn_sem, kv_sem, xown_sem, ps_send, ps_recv, rs_send, rs_recv, ag_send, ag_recv,
                 yl_sem, yp_send, yp_recv, credit):
    tokens, width, ff, fpad, q_cols, kv_heads, tp_size = cfg
    blocks = ROW_BLOCKS
    rows = tokens // blocks
    ring = tp_size // 2
    k_w = width // K_STEPS
    n_w = width // N_STEPS
    half = width // 2
    c_w = half // (2 * ring)
    per_n = n_w // c_w
    s_rows = rows // SUBS
    q_local = q_cols // HEAD_DIM
    scale = 1.0 / math.sqrt(HEAD_DIM)
    f32, bf16 = jnp.float32, jnp.bfloat16

    me = lax.axis_index('tp')
    pos, core = me // 2, me % 2
    nxt = (lax.rem(pos + 1, ring) * 2 + core, lax.rem(pos + ring - 1, ring) * 2 + core)
    partner = pos * 2 + (1 - core)
    head_col = pl.multiple_of(me * kv_heads // tp_size * HEAD_DIM, HEAD_DIM)

    barrier = pltpu.get_barrier_semaphore()
    for other in (nxt[0], nxt[1], partner):
        pl.semaphore_signal(barrier, inc=1, device_id={'tp': other}, device_id_type=MESH)
    pl.semaphore_wait(barrier, 3)

    def x_copy(b):
        return pltpu.make_async_copy(x_hbm.at[pl.ds(pl.multiple_of(b * rows, rows), rows)], xbuf, x_sem)

    def k_copies(k):
        s = lax.rem(k, 3)
        lo = pl.multiple_of(k * k_w, k_w)
        return (
            pltpu.make_async_copy(wg_hbm.at[:, pl.ds(lo, k_w)], wgu.at[s, pl.ds(0, ff)], wk_sem.at[s, 0]),
            pltpu.make_async_copy(wu_hbm.at[:, pl.ds(lo, k_w)], wgu.at[s, pl.ds(fpad, ff)], wk_sem.at[s, 1]),
            pltpu.make_async_copy(wq_hbm.at[pl.ds(lo, k_w)], wqkv.at[s, :, pl.ds(0, q_cols)], wk_sem.at[s, 2]),
            pltpu.make_async_copy(wk_hbm.at[pl.ds(lo, k_w), pl.ds(head_col, HEAD_DIM)],
                                  wqkv.at[s, :, pl.ds(q_cols, HEAD_DIM)], wk_sem.at[s, 3]),
            pltpu.make_async_copy(wv_hbm.at[pl.ds(lo, k_w), pl.ds(head_col, HEAD_DIM)],
                                  wqkv.at[s, :, pl.ds(q_cols + HEAD_DIM, HEAD_DIM)], wk_sem.at[s, 4]),
        )

    def n_copies(n):
        s = lax.rem(n, 3)
        piece = n // (N_STEPS // 2)
        side = jnp.where(piece == 0, 1 - core, core)
        lo = pl.multiple_of(side * half + lax.rem(n, N_STEPS // 2) * n_w, n_w)
        return (
            pltpu.make_async_copy(wo_hbm.at[:, pl.ds(lo, n_w)], wo_buf.at[s], wn_sem.at[s, 0]),
            pltpu.make_async_copy(wd_hbm.at[:, pl.ds(lo, n_w)], wd_buf.at[s, pl.ds(0, ff)], wn_sem.at[s, 1]),
        )

    def start(copies):
        for copy in copies:
            copy.start()

    def wait(copies):
        for copy in copies:
            copy.wait()

    def kv_copies(b):
        r = pl.ds(pl.multiple_of(b * rows, rows), rows)
        return (pltpu.make_async_copy(k_buf.at[r], k_hbm.at[r], kv_sem.at[0]),
                pltpu.make_async_copy(v_buf.at[r], v_hbm.at[r], kv_sem.at[1]))

    def xown_copies(b):
        out = []
        for d in range(2):
            col = pl.multiple_of(core * half + (d * ring + pos) * c_w, c_w)
            out.append(pltpu.make_async_copy(
                x_hbm.at[pl.ds(pl.multiple_of(b * rows, rows), rows), pl.ds(col, c_w)],
                xown.at[lax.rem(b, 2), d], xown_sem.at[lax.rem(b, 2), d]))
        return out

    def ps_copy(b, n):
        part = pl.ds(n * per_n, per_n)
        return pltpu.make_async_remote_copy(
            pbuf.at[0, part], precv.at[lax.rem(b, 2), part], ps_send, ps_recv.at[lax.rem(b, 2)],
            device_id={'tp': partner}, device_id_type=MESH)

    def rs_copy(src, b, d, s, sub):
        par = lax.rem(b, 2)
        return pltpu.make_async_remote_copy(
            src, rsbuf.at[par, d, s, sub], rs_send, rs_recv.at[par, d, s, sub],
            device_id={'tp': nxt[d]}, device_id_type=MESH)

    def ag_copy(b, d, s, k, sub):
        ref = ybuf.at[b, d * ring + k, sub]
        return pltpu.make_async_remote_copy(
            ref, ref, ag_send.at[b], ag_recv.at[b, d, s, sub], device_id={'tp': nxt[d]}, device_id_type=MESH)

    def put_out(b, d, k, sub):
        src = ybuf.at[b, d * ring + k, sub]
        r = pl.multiple_of(b * rows + sub * s_rows, s_rows)
        col = pl.multiple_of(core * half + (d * ring + k) * c_w, c_w)
        dst = y_hbm.at[pl.ds(r, s_rows), pl.ds(col, c_w)]
        pltpu.make_async_copy(src, dst, yl_sem.at[b]).start()
        pltpu.make_async_remote_copy(src, dst, yp_send.at[b], yp_recv.at[b],
                                     device_id={'tp': partner}, device_id_type=MESH).start()

    def own_share(b, d, k, sub):
        par = lax.rem(b, 2)
        q = d * ring + k
        return pbuf[1 + par, q, sub].astype(f32) + precv[par, q, sub].astype(f32)

    def rs_step(b, s, sub):
        par = lax.rem(b, 2)
        for d in range(2):
            k = lax.rem(pos + 2 * ring - 1 - s, ring) if d == 0 else lax.rem(pos + 1 + s, ring)

            @pl.when(s == 0)
            def _():
                src = pbuf.at[1 + par, d * ring + k, sub]
                src[...] = own_share(b, d, k, sub).astype(bf16)
                rs_copy(src, b, d, s, sub).start()

            @pl.when(s > 0)
            def _():
                src = rsbuf.at[par, d, s - 1, sub]
                rs_copy(src, b, d, s - 1, sub).wait_recv()
                src[...] = (own_share(b, d, k, sub) + src[...].astype(f32)).astype(bf16)
                rs_copy(src, b, d, s, sub).start()

    def ag_step(b, s, sub):
        par = lax.rem(b, 2)

        @pl.when((s == 0) & (sub == 0))
        def _():
            wait(xown_copies(b))

        for d in range(2):
            k = lax.rem(pos + ring - s, ring) if d == 0 else lax.rem(pos + s, ring)

            @pl.when(s == 0)
            def _():
                last = rsbuf.at[par, d, ring - 2, sub]
                rs_copy(last, b, d, ring - 2, sub).wait_recv()
                total = own_share(b, d, k, sub) + last[...].astype(f32)
                r = pl.ds(pl.multiple_of(sub * s_rows, s_rows), s_rows)
                ybuf[b, d * ring + k, sub] = (xown[par, d, r].astype(f32) + total).astype(bf16)

            @pl.when(s > 0)
            def _():
                ag_copy(b, d, s - 1, k, sub).wait_recv()

            ag_copy(b, d, s, k, sub).start()
            put_out(b, d, k, sub)

    def ag_last(b, sub):
        for d in range(2):
            k = lax.rem(pos + 1, ring) if d == 0 else lax.rem(pos + ring - 1, ring)
            ag_copy(b, d, ring - 2, k, sub).wait_recv()
            put_out(b, d, k, sub)

    def comm(t, j):
        s, sub = j // SUBS, lax.rem(j, SUBS)

        @pl.when((s == 0) & (t >= 3))
        def _():
            ag_last(t - 3, sub)

        @pl.when((t >= 1) & (t <= blocks))
        def _():
            rs_step(t - 1, s, sub)

        @pl.when((t >= 2) & (t <= blocks + 1))
        def _():
            ag_step(t - 2, s, sub)

        @pl.when((j == SUBS) & (t >= 2) & (t < blocks))
        def _():
            pl.semaphore_signal(credit, inc=1, device_id={'tp': partner}, device_id_type=MESH)

    def norm_rows(i, carry):
        r = pl.ds(pl.multiple_of(i * 16, 16), 16)
        x32 = xbuf[r].astype(f32)
        inv = lax.rsqrt(jnp.mean(x32 * x32, axis=-1, keepdims=True) + NORM_EPS)
        a_buf[r] = (x32 * inv * g_ref[...].astype(f32)).astype(bf16)
        return carry

    def k_step(k):
        s = lax.rem(k, 3)
        wait(k_copies(k))

        @pl.when(k + 2 < K_STEPS)
        def _():
            start(k_copies(k + 2))

        @pl.when(k + 2 >= K_STEPS)
        def _():
            start(n_copies(k + 2 - K_STEPS))

        a_k = a_buf[:, pl.ds(pl.multiple_of(k * k_w, k_w), k_w)]
        for lo in range(0, 2 * fpad, 512):
            hi = min(lo + 512, 2 * fpad)
            acc_gu[:, lo:hi] += lax.dot_general(a_k, wgu[s, lo:hi], (((1,), (1,)), ((), ())), preferred_element_type=f32)
        acc_qkv[...] += jnp.dot(a_k, wqkv[s], preferred_element_type=f32)

    def rope(v, t):
        r = pl.ds(pl.multiple_of(t * rows, rows), rows)
        return v * cos_ref[r] + pltpu.roll(v, HEAD_DIM // 2, 1) * sin_ref[r]

    def attend(t, h):
        r = pl.ds(pl.multiple_of(t * rows, rows), rows)
        if h == 0:
            k_buf[r] = rope(acc_qkv[:, q_cols:q_cols + HEAD_DIM], t).astype(bf16)
            v_buf[r] = acc_qkv[:, q_cols + HEAD_DIM:q_cols + 2 * HEAD_DIM].astype(bf16)
            start(kv_copies(t))
            start(n_copies(2))
        span = slice(h * HEAD_DIM, (h + 1) * HEAD_DIM)
        q_rot = rope(acc_qkv[:, span], t).astype(bf16)
        scores = lax.dot_general(q_rot, k_buf[...], (((1,), (1,)), ((), ())), preferred_element_type=f32) * scale
        row_id = t * rows + lax.broadcasted_iota(jnp.int32, scores.shape, 0)
        col_id = lax.broadcasted_iota(jnp.int32, scores.shape, 1)
        scores = jnp.where(col_id <= row_id, scores, -1e30)
        expd = jnp.exp(scores - jnp.max(scores, axis=-1, keepdims=True))
        probs = (expd / jnp.sum(expd, axis=-1, keepdims=True)).astype(bf16)
        o_buf[:, span] = jnp.dot(probs, v_buf[...], preferred_element_type=f32).astype(bf16)
        q_rows = rows // q_local
        part = slice(h * q_rows, (h + 1) * q_rows)
        gate = acc_gu[part, 0:fpad]
        m_buf[part] = (gate * (1.0 / (1.0 + jnp.exp(-gate))) * acc_gu[part, fpad:2 * fpad]).astype(bf16)

    def n_step(t, n):
        s = lax.rem(n, 3)
        wait(n_copies(n))

        @pl.when((n >= 1) & (n + 2 < N_STEPS))
        def _():
            start(n_copies(n + 2))

        @pl.when((n + 2 >= N_STEPS) & (t + 1 < blocks))
        def _():
            start(k_copies(n + 2 - N_STEPS))

        @pl.when((n == 0) & (t >= 2))
        def _():
            pl.semaphore_wait(credit, 1)

        mine = n >= N_STEPS // 2
        slot = jnp.where(mine, 1 + lax.rem(t, 2), 0)
        piece = lax.rem(n, N_STEPS // 2)
        o_v, m_v = o_buf[...], m_buf[...]
        for i in range(per_n):
            cols = slice(i * c_w, (i + 1) * c_w)
            out = (jnp.dot(o_v, wo_buf[s, :, cols], preferred_element_type=f32)
                   + jnp.dot(m_v, wd_buf[s, :, cols], preferred_element_type=f32)).astype(bf16)
            pbuf[slot, piece * per_n + i] = out.reshape(SUBS, s_rows, c_w)

        @pl.when(jnp.logical_not(mine))
        def _():
            ps_copy(t, piece).start()

    x_copy(0).start()
    start(k_copies(0))
    start(k_copies(1))
    wgu[:, ff:fpad] = jnp.zeros((3, fpad - ff, k_w), bf16)
    wgu[:, fpad + ff:] = jnp.zeros((3, fpad - ff, k_w), bf16)
    wd_buf[:, ff:] = jnp.zeros((3, fpad - ff, n_w), bf16)
    k_buf[...] = jnp.zeros(k_buf.shape, bf16)
    v_buf[...] = jnp.zeros(v_buf.shape, bf16)

    def slot_body(t, carry):
        computes = t < blocks
        sends = (t >= 1) & (t <= blocks)

        @pl.when(sends)
        def _():
            pltpu.make_async_copy(precv.at[lax.rem(t - 1, 2)], precv.at[lax.rem(t - 1, 2)],
                                  ps_recv.at[lax.rem(t - 1, 2)]).wait()
            start(xown_copies(t - 1))

        @pl.when(computes)
        def _():
            x_copy(t).wait()
            lax.fori_loop(0, rows // 16, norm_rows, 0)

            @pl.when(t + 1 < blocks)
            def _():
                x_copy(t + 1).start()

            acc_gu[...] = jnp.zeros(acc_gu.shape, f32)
            acc_qkv[...] = jnp.zeros(acc_qkv.shape, f32)

        def k_body(k, c):
            comm(t, k)

            @pl.when(computes)
            def _():
                k_step(k)
            return c

        lax.fori_loop(0, K_STEPS, k_body, 0)
        for h in range(q_local):
            comm(t, K_STEPS + h)

            @pl.when(computes)
            def _():
                attend(t, h)

        def n_body(n, c):
            comm(t, K_STEPS + q_local + n)

            @pl.when(computes)
            def _():
                n_step(t, n)
            return c

        lax.fori_loop(0, N_STEPS, n_body, 0)

        @pl.when(sends)
        def _():
            pltpu.make_async_copy(rsbuf.at[0], rsbuf.at[0], rs_send).wait()

        @pl.when(computes)
        def _():
            pltpu.make_async_copy(pbuf.at[0], pbuf.at[0], ps_send).wait()
            wait(kv_copies(t))
        return carry

    lax.fori_loop(0, blocks + 2, slot_body, 0)
    for sub in range(SUBS):
        ag_last(blocks - 1, sub)
    for b in range(blocks):
        whole, sent = ybuf.at[b], ybuf.at[b, pl.ds(0, 2 * (ring - 1))]
        pltpu.make_async_copy(sent, sent, ag_send.at[b]).wait()
        for sem in (yl_sem, yp_send, yp_recv):
            pltpu.make_async_copy(whole, whole, sem.at[b]).wait()


def solution(mesh):
    tp_size = mesh.shape['tp']

    def local_layer(x_in, g_norm, w_q, w_k, w_v, w_o, w_gate, w_up, w_down):
        tokens, width = x_in.shape
        ff, q_cols = w_gate.shape[1], w_q.shape[1]
        kv_heads = w_k.shape[1] // HEAD_DIM
        fpad = round_up(ff, HEAD_DIM)
        rows, ring = tokens // ROW_BLOCKS, tp_size // 2
        k_w, n_w = width // K_STEPS, width // N_STEPS
        c_w = width // (4 * ring)
        s_rows = rows // SUBS
        assert K_STEPS + q_cols // HEAD_DIM + N_STEPS == SUBS * (ring - 1)
        cos_tab, sin_tab = rope_tables(jnp.arange(tokens))
        cos_full = jnp.concatenate([cos_tab, cos_tab], axis=1)
        sin_full = jnp.concatenate([-sin_tab, sin_tab], axis=1)
        cfg = (tokens, width, ff, fpad, q_cols, kv_heads, tp_size)
        bf16, f32 = jnp.bfloat16, jnp.float32
        dma, vmem = pltpu.SemaphoreType.DMA, pltpu.VMEM
        any_spec, vmem_spec = pl.BlockSpec(memory_space=pl.ANY), pl.BlockSpec(memory_space=pltpu.VMEM)
        blocks = ROW_BLOCKS
        y_out, k_out, v_out = pl.pallas_call(
            functools.partial(layer_kernel, cfg),
            out_shape=(jax.ShapeDtypeStruct((tokens, width), bf16),
                       jax.ShapeDtypeStruct((tokens, HEAD_DIM), bf16),
                       jax.ShapeDtypeStruct((tokens, HEAD_DIM), bf16)),
            in_specs=[any_spec, vmem_spec, vmem_spec, vmem_spec] + [any_spec] * 7,
            out_specs=(any_spec,) * 3,
            scratch_shapes=[
                vmem((rows, width), bf16),
                vmem((rows, width), bf16),
                vmem((3, 2 * fpad, k_w), bf16),
                vmem((3, k_w, q_cols + 2 * HEAD_DIM), bf16),
                vmem((3, q_cols, n_w), bf16),
                vmem((3, fpad, n_w), bf16),
                vmem((rows, 2 * fpad), f32),
                vmem((rows, q_cols + 2 * HEAD_DIM), f32),
                vmem((rows, fpad), bf16),
                vmem((rows, q_cols), bf16),
                vmem((rows, HEAD_DIM), bf16),
                vmem((tokens, HEAD_DIM), bf16),
                vmem((tokens, HEAD_DIM), bf16),
                vmem((3, 2 * ring, SUBS, s_rows, c_w), bf16),
                vmem((2, 2 * ring, SUBS, s_rows, c_w), bf16),
                vmem((2, 2, ring - 1, SUBS, s_rows, c_w), bf16),
                vmem((blocks, 2 * ring, SUBS, s_rows, c_w), bf16),
                vmem((2, 2, rows, c_w), bf16),
                dma, dma((3, 5)), dma((3, 2)), dma((2,)), dma((2, 2)),
                dma, dma((2,)), dma, dma((2, 2, ring - 1, SUBS)),
                dma((blocks,)), dma((blocks, 2, ring - 1, SUBS)),
                dma((blocks,)), dma((blocks,)), dma((blocks,)),
                pltpu.SemaphoreType.REGULAR,
            ],
            compiler_params=pltpu.CompilerParams(collective_id=0, has_side_effects=True, vmem_limit_bytes=67043328),
        )(x_in, g_norm.reshape(1, width), cos_full, sin_full, w_q, w_k, w_v, w_o, w_gate.T, w_up.T, w_down)
        return y_out, k_out.reshape(tokens, 1, HEAD_DIM), v_out.reshape(tokens, 1, HEAD_DIM)

    return jax.shard_map(local_layer, mesh=mesh, in_specs=(P('dp', None), P(None), P(None, 'tp'), P(None, None), P(None, None), P('tp', None), P(None, 'tp'), P(None, 'tp'), P('tp', None)), out_specs=(P('dp', None), P('dp', 'tp', None), P('dp', 'tp', None)), check_vma=False)
```

time: 708 us -> 272 us (0.38)
  matrix products: 431 us -> 0 us
  Pallas kernels: 0 us -> 251 us
  waiting for transfers between devices: 197 us -> 0 us
  other arithmetic: 50.4 us -> 3.22 us
  between operations: 14.2 us -> 0.67 us
  local copies, waits for them, and re-layouts: 8.61 us -> 16.8 us
    dot_general x50 -> x0, matrix products: 431 us -> none  [the longest x8 208 us: row_block(): jnp.dot(hidden, w_down, preferred_element_type=jnp.float32)]
    pallas_call x0 -> x1, Pallas kernels: none -> 251 us  [local_layer(): pl.pallas_call(functools.partial(layer_kernel, cfg), out_shape=(jax.Shape...]
    psum x1 -> x0, waiting for transfers between devices: 197 us -> none  [local_layer(): reduced_sum = lax.psum(partial_sum, 'tp')]
    convert_element_type x3 -> x0, other arithmetic: 34.2 us -> none  [the longest x1 18.2 us: local_layer(): (x_in.astype(jnp.float32) + reduced_sum.astype(jnp.float32)).astype(jnp.b...]
    unnamed x6 -> x7, local copies, waits for them, and re-layouts: 0.85 us -> 15.4 us
    reduce_sum x9 -> x0, other arithmetic: 11.4 us -> none  [the longest x1 7.18 us: rms_norm(): jnp.mean(x_f32 * x_f32, axis=-1, keepdims=True) + NORM_EPS]
  transfers between devices with their start and end apart: 1 -> 0, of which waited for: 1 -> 0; matrix products, arithmetic and copies ran while one was open for 0% -> 0% of each run, Pallas kernels for 0% -> 0%
where the time goes in v1:
time: 272 us
  Pallas kernels  251 us (92%)
  local copies, waits for them, and re-layouts  16.8 us (6%)
  other arithmetic  3.22 us (1%)
    pallas_call x1, Pallas kernels, local_layer(): pl.pallas_call(functools.partial(layer_kernel, cfg), out_shape=(jax.Shape...  251 us
    unnamed x7, local copies, waits for them, and re-layouts  15.4 us

profile of v1, /device:TPU:21, one launch (start us, length us, event | category | flops | bytes accessed | tf_op | source)
XLA Modules:
  0.0 271.6 jit_solution(10651789546498605574)
XLA Ops:
  0.7 1.4 reshape.26.g_ref
  2.0 1.9 fusion
  3.9 1.3 pad_maximum_fusion
  5.2 250.9 %shard_map.112 = (bf16[1024,8192]{1,0:T(8,128)(2,1)}, bf16[1024,128]{1,0:T(8,128)(2,1)}, bf16[1024,128]{1,0:T(8,128)(2,1)}) custom-call(bf16[1024,8192]{1,0:T(8,128)(2,1)} %x_hbm.1, bf16[1,8192]{1,0:T(2,128)(2,1)} %reshape.26.g_ref, f32[1024,128]{1,0:T(8,128)} %get-tuple-element.12.cos_ref, f32[1024,128]{1,0:T(8,128)} %get-tuple-element.13.sin_ref, ...), custom_call_target="tpu_custom_call" | custom-call | tf_op jit(solution)/shard_map/pallas_call | solution.py:387
  256.1 0.0 copy-start.1
  256.1 0.0 copy-start
  256.1 14.0 %copy.15 = bf16[1024,8192]{1,0:T(8,128)(2,1)} copy(bf16[1024,8192]{1,0:T(8,128)(2,1)} %get-tuple-element.17) | data formatting | bytes 33554432
  270.1 0.0 copy-done.1
  270.1 0.7 copy.16
  270.9 0.0 copy-done
  270.9 0.7 copy.17
  (2 shorter events, 0.0 us)
Async XLA Ops:
  256.1 14.0 %copy-start.1 = (bf16[1024,128]{1,0:T(8,128)(2,1)S(1)}, bf16[1024,128]{1,0:T(8,128)(2,1)}, u32[]{:S(2)}) copy-start(bf16[1024,128]{1,0:T(8,128)(2,1)} %get-tuple-element.7) | copy-start | bytes 786436
  256.1 14.7 %copy-start = (bf16[1024,128]{1,0:T(8,128)(2,1)S(1)}, bf16[1024,128]{1,0:T(8,128)(2,1)}, u32[]{:S(2)}) copy-start(bf16[1024,128]{1,0:T(8,128)(2,1)} %get-tuple-element.8) | copy-start | bytes 786436

commit v2 on v1

--- a/solution.py
+++ b/solution.py
@@ -2,6 +2,7 @@
 import math
 import jax
 import jax.numpy as jnp
+import numpy as np
 from jax import lax
 from jax.experimental import pallas as pl
 from jax.experimental.pallas import tpu as pltpu
@@ -18,10 +19,11 @@
 MESH = pl.DeviceIdType.MESH
 
 
-def rope_tables(positions):
-    inv_freq = ROPE_BASE ** (-jnp.arange(0, HEAD_DIM, 2, dtype=jnp.float32) / HEAD_DIM)
-    angles = positions.astype(jnp.float32)[:, None] * inv_freq[None, :]
-    return jnp.cos(angles), jnp.sin(angles)
+def rope_tables(tokens):
+    inv_freq = np.float32(ROPE_BASE) ** (-np.arange(0, HEAD_DIM, 2, dtype=np.float32) / np.float32(HEAD_DIM))
+    angles = (np.arange(tokens, dtype=np.float32)[:, None] * inv_freq[None, :].astype(np.float32)).astype(np.float64)
+    cos_tab, sin_tab = np.cos(angles).astype(np.float32), np.sin(angles).astype(np.float32)
+    return np.concatenate([cos_tab, cos_tab], axis=1), np.concatenate([-sin_tab, sin_tab], axis=1)
 
 
 def round_up(n, m):
@@ -30,7 +32,7 @@
 
 def layer_kernel(cfg, x_hbm, g_ref, cos_ref, sin_ref, wq_hbm, wk_hbm, wv_hbm, wo_hbm, wg_hbm, wu_hbm, wd_hbm,
                  y_hbm, k_hbm, v_hbm,
-                 xbuf, a_buf, wgu, wqkv, wo_buf, wd_buf, acc_gu, acc_qkv, m_buf, o_buf, q_buf, k_buf, v_buf,
+                 xbuf, a_buf, wgu, wqkv, wo_buf, wd_buf, acc_gu, acc_qkv, m_buf, o_buf, k_buf, v_buf,
                  pbuf, precv, rsbuf, ybuf, xown,
                  x_sem, wk_sem, wn_sem, kv_sem, xown_sem, ps_send, ps_recv, rs_send, rs_recv, ag_send, ag_recv,
                  yl_sem, yp_send, yp_recv, credit):
@@ -120,23 +122,25 @@
             device_id={'tp': nxt[d]}, device_id_type=MESH)
 
     def ag_copy(b, d, s, k, sub):
-        ref = ybuf.at[b, d * ring + k, sub]
+        ref = ybuf.at[b, d * ring + k, sub_rows(sub)]
         return pltpu.make_async_remote_copy(
             ref, ref, ag_send.at[b], ag_recv.at[b, d, s, sub], device_id={'tp': nxt[d]}, device_id_type=MESH)
 
-    def put_out(b, d, k, sub):
-        src = ybuf.at[b, d * ring + k, sub]
-        r = pl.multiple_of(b * rows + sub * s_rows, s_rows)
+    def put_out(b, d, k):
+        src = ybuf.at[b, d * ring + k]
         col = pl.multiple_of(core * half + (d * ring + k) * c_w, c_w)
-        dst = y_hbm.at[pl.ds(r, s_rows), pl.ds(col, c_w)]
+        dst = y_hbm.at[pl.ds(pl.multiple_of(b * rows, rows), rows), pl.ds(col, c_w)]
         pltpu.make_async_copy(src, dst, yl_sem.at[b]).start()
         pltpu.make_async_remote_copy(src, dst, yp_send.at[b], yp_recv.at[b],
                                      device_id={'tp': partner}, device_id_type=MESH).start()
 
+    def sub_rows(sub):
+        return pl.ds(pl.multiple_of(sub * s_rows, s_rows), s_rows)
+
     def own_share(b, d, k, sub):
         par = lax.rem(b, 2)
         q = d * ring + k
-        return pbuf[1 + par, q, sub].astype(f32) + precv[par, q, sub].astype(f32)
+        return pbuf[1 + par, q, sub_rows(sub)].astype(f32) + precv[par, q, sub_rows(sub)].astype(f32)
 
     def rs_step(b, s, sub):
         par = lax.rem(b, 2)
@@ -145,7 +149,7 @@
 
             @pl.when(s == 0)
             def _():
-                src = pbuf.at[1 + par, d * ring + k, sub]
+                src = pbuf.at[1 + par, d * ring + k, sub_rows(sub)]
                 src[...] = own_share(b, d, k, sub).astype(bf16)
                 rs_copy(src, b, d, s, sub).start()
 
@@ -171,21 +175,27 @@
                 last = rsbuf.at[par, d, ring - 2, sub]
                 rs_copy(last, b, d, ring - 2, sub).wait_recv()
                 total = own_share(b, d, k, sub) + last[...].astype(f32)
-                r = pl.ds(pl.multiple_of(sub * s_rows, s_rows), s_rows)
-                ybuf[b, d * ring + k, sub] = (xown[par, d, r].astype(f32) + total).astype(bf16)
+                r = sub_rows(sub)
+                ybuf[b, d * ring + k, r] = (xown[par, d, r].astype(f32) + total).astype(bf16)
 
             @pl.when(s > 0)
             def _():
                 ag_copy(b, d, s - 1, k, sub).wait_recv()
 
             ag_copy(b, d, s, k, sub).start()
-            put_out(b, d, k, sub)
+
+            @pl.when(sub == SUBS - 1)
+            def _():
+                put_out(b, d, k)
 
     def ag_last(b, sub):
         for d in range(2):
             k = lax.rem(pos + 1, ring) if d == 0 else lax.rem(pos + ring - 1, ring)
             ag_copy(b, d, ring - 2, k, sub).wait_recv()
-            put_out(b, d, k, sub)
+
+            @pl.when(sub == SUBS - 1)
+            def _():
+                put_out(b, d, k)
 
     def comm(t, j):
         s, sub = j // SUBS, lax.rem(j, SUBS)
@@ -206,18 +216,18 @@
         def _():
             pl.semaphore_signal(credit, inc=1, device_id={'tp': partner}, device_id_type=MESH)
 
-    def norm_rows(i, carry):
+    def norm_rows(i, carry=0):
         r = pl.ds(pl.multiple_of(i * 16, 16), 16)
         x32 = xbuf[r].astype(f32)
         inv = lax.rsqrt(jnp.mean(x32 * x32, axis=-1, keepdims=True) + NORM_EPS)
         a_buf[r] = (x32 * inv * g_ref[...].astype(f32)).astype(bf16)
         return carry
 
-    def k_step(k):
+    def k_step(t, k):
         s = lax.rem(k, 3)
         wait(k_copies(k))
 
-        @pl.when(k + 2 < K_STEPS)
+        @pl.when((k + 2 < K_STEPS) & ((k > 0) | (t > 0)))
         def _():
             start(k_copies(k + 2))
 
@@ -272,28 +282,36 @@
         def _():
             pl.semaphore_wait(credit, 1)
 
+        @pl.when((n == 0) & (t + 1 < blocks))
+        def _():
+            x_copy(t + 1).wait()
+
         mine = n >= N_STEPS // 2
         slot = jnp.where(mine, 1 + lax.rem(t, 2), 0)
         piece = lax.rem(n, N_STEPS // 2)
+        for i in range(rows // (16 * N_STEPS)):
+            norm_rows(n * (rows // (16 * N_STEPS)) + i)
         o_v, m_v = o_buf[...], m_buf[...]
         for i in range(per_n):
             cols = slice(i * c_w, (i + 1) * c_w)
             out = (jnp.dot(o_v, wo_buf[s, :, cols], preferred_element_type=f32)
                    + jnp.dot(m_v, wd_buf[s, :, cols], preferred_element_type=f32)).astype(bf16)
-            pbuf[slot, piece * per_n + i] = out.reshape(SUBS, s_rows, c_w)
+            pbuf[slot, piece * per_n + i] = out
 
         @pl.when(jnp.logical_not(mine))
         def _():
             ps_copy(t, piece).start()
 
     x_copy(0).start()
-    start(k_copies(0))
-    start(k_copies(1))
     wgu[:, ff:fpad] = jnp.zeros((3, fpad - ff, k_w), bf16)
     wgu[:, fpad + ff:] = jnp.zeros((3, fpad - ff, k_w), bf16)
     wd_buf[:, ff:] = jnp.zeros((3, fpad - ff, n_w), bf16)
     k_buf[...] = jnp.zeros(k_buf.shape, bf16)
     v_buf[...] = jnp.zeros(v_buf.shape, bf16)
+    x_copy(0).wait()
+    for k in range(3):
+        start(k_copies(k))
+    lax.fori_loop(0, rows // 16, norm_rows, 0)
 
     def slot_body(t, carry):
         computes = t < blocks
@@ -307,9 +325,6 @@
 
         @pl.when(computes)
         def _():
-            x_copy(t).wait()
-            lax.fori_loop(0, rows // 16, norm_rows, 0)
-
             @pl.when(t + 1 < blocks)
             def _():
                 x_copy(t + 1).start()
@@ -322,7 +337,7 @@
 
             @pl.when(computes)
             def _():
-                k_step(k)
+                k_step(t, k)
             return c
 
         lax.fori_loop(0, K_STEPS, k_body, 0)
@@ -361,6 +376,23 @@
         pltpu.make_async_copy(sent, sent, ag_send.at[b]).wait()
         for sem in (yl_sem, yp_send, yp_recv):
             pltpu.make_async_copy(whole, whole, sem.at[b]).wait()
+
+
+def copy_kernel(pieces, y_in, k_in, v_in, y_out, k_out, v_out, y_buf, kv_buf, in_sem, out_sem):
+    tokens = y_in.shape[0]
+    piece = tokens // pieces
+    moves = [(y_in.at[pl.ds(i * piece, piece)], y_buf.at[pl.ds(i * piece, piece)], y_out.at[pl.ds(i * piece, piece)])
+             for i in range(pieces)]
+    moves += [(k_in, kv_buf.at[0], k_out), (v_in, kv_buf.at[1], v_out)]
+    ins = [pltpu.make_async_copy(src, mid, in_sem.at[i]) for i, (src, mid, _) in enumerate(moves)]
+    outs = [pltpu.make_async_copy(mid, dst, out_sem.at[i]) for i, (_, mid, dst) in enumerate(moves)]
+    for copy in ins:
+        copy.start()
+    for arrived, leaving in zip(ins, outs):
+        arrived.wait()
+        leaving.start()
+    for copy in outs:
+        copy.wait()
 
 
 def solution(mesh):
@@ -375,10 +407,9 @@
         k_w, n_w = width // K_STEPS, width // N_STEPS
         c_w = width // (4 * ring)
         s_rows = rows // SUBS
+        assert rows % (16 * N_STEPS) == 0
         assert K_STEPS + q_cols // HEAD_DIM + N_STEPS == SUBS * (ring - 1)
-        cos_tab, sin_tab = rope_tables(jnp.arange(tokens))
-        cos_full = jnp.concatenate([cos_tab, cos_tab], axis=1)
-        sin_full = jnp.concatenate([-sin_tab, sin_tab], axis=1)
+        cos_full, sin_full = (jnp.asarray(table) for table in rope_tables(tokens))
         cfg = (tokens, width, ff, fpad, q_cols, kv_heads, tp_size)
         bf16, f32 = jnp.bfloat16, jnp.float32
         dma, vmem = pltpu.SemaphoreType.DMA, pltpu.VMEM
@@ -402,13 +433,12 @@
                 vmem((rows, q_cols + 2 * HEAD_DIM), f32),
                 vmem((rows, fpad), bf16),
                 vmem((rows, q_cols), bf16),
-                vmem((rows, HEAD_DIM), bf16),
                 vmem((tokens, HEAD_DIM), bf16),
                 vmem((tokens, HEAD_DIM), bf16),
-                vmem((3, 2 * ring, SUBS, s_rows, c_w), bf16),
-                vmem((2, 2 * ring, SUBS, s_rows, c_w), bf16),
+                vmem((3, 2 * ring, rows, c_w), bf16),
+                vmem((2, 2 * ring, rows, c_w), bf16),
                 vmem((2, 2, ring - 1, SUBS, s_rows, c_w), bf16),
-                vmem((blocks, 2 * ring, SUBS, s_rows, c_w), bf16),
+                vmem((blocks, 2 * ring, rows, c_w), bf16),
                 vmem((2, 2, rows, c_w), bf16),
                 dma, dma((3, 5)), dma((3, 2)), dma((2,)), dma((2, 2)),
                 dma, dma((2,)), dma, dma((2, 2, ring - 1, SUBS)),
@@ -418,6 +448,17 @@
             ],
             compiler_params=pltpu.CompilerParams(collective_id=0, has_side_effects=True, vmem_limit_bytes=67043328),
         )(x_in, g_norm.reshape(1, width), cos_full, sin_full, w_q, w_k, w_v, w_o, w_gate.T, w_up.T, w_down)
+        pieces = 32
+        shapes = (y_out, k_out, v_out)
+        y_out, k_out, v_out = pl.pallas_call(
+            functools.partial(copy_kernel, pieces),
+            out_shape=tuple(jax.ShapeDtypeStruct(v.shape, v.dtype) for v in shapes),
+            in_specs=[any_spec] * 3,
+            out_specs=(any_spec,) * 3,
+            scratch_shapes=[vmem((tokens, width), bf16), vmem((2, tokens, HEAD_DIM), bf16),
+                            dma((pieces + 2,)), dma((pieces + 2,))],
+            compiler_params=pltpu.CompilerParams(vmem_limit_bytes=67043328),
+        )(*shapes)
         return y_out, k_out.reshape(tokens, 1, HEAD_DIM), v_out.reshape(tokens, 1, HEAD_DIM)
 
     return jax.shard_map(local_layer, mesh=mesh, in_specs=(P('dp', None), P(None), P(None, 'tp'), P(None, None), P(None, None), P('tp', None), P(None, 'tp'), P(None, 'tp'), P('tp', None)), out_specs=(P('dp', None), P('dp', 'tp', None), P('dp', 'tp', None)), check_vma=False)

time: 272 us -> 255 us (0.938)
  local copies, waits for them, and re-layouts: 16.8 us -> 1.35 us
  other arithmetic: 3.22 us -> 0 us
    unnamed x7 -> x0, local copies, waits for them, and re-layouts: 15.4 us -> none
    pallas_call x0 -> x1, Pallas kernels: none -> 12.5 us  [local_layer(): pl.pallas_call(functools.partial(copy_kernel, pieces), out_shape=tuple((j...]
    pallas_call x1, Pallas kernels: 251 us -> 240 us  [local_layer(): pl.pallas_call(functools.partial(layer_kernel, cfg), out_shape=(jax.Shape...]
where the time goes in v2:
time: 255 us; the launch traced here: 254 us
  Pallas kernels  252 us (99%)
    pallas_call x1, Pallas kernels, local_layer(): pl.pallas_call(functools.partial(layer_kernel, cfg), out_shape=(jax.Shape...  240 us
    pallas_call x1, Pallas kernels, local_layer(): pl.pallas_call(functools.partial(copy_kernel, pieces), out_shape=tuple((j...  12.5 us

profile of v2, /device:TPU:21, one launch (start us, length us, event | category | flops | bytes accessed | tf_op | source)
XLA Modules:
  0.0 254.4 jit_solution(15779037145585869949)
XLA Ops:
  0.6 1.4 reshape.15.g_ref
  2.0 239.9 %shard_map.130 = (bf16[1024,8192]{1,0:T(8,128)(2,1)}, bf16[1024,128]{1,0:T(8,128)(2,1)}, bf16[1024,128]{1,0:T(8,128)(2,1)}) custom-call(bf16[1024,8192]{1,0:T(8,128)(2,1)} %x_hbm.1, bf16[1,8192]{1,0:T(2,128)(2,1)} %reshape.15.g_ref, f32[1024,128]{1,0:T(8,128)} %constant.4.clone.cos_ref, f32[1024,128]{1,0:T(8,128)} %constant.5.clone.sin_ref, ...), custom_call_target="tpu_custom_call" | custom-call | tf_op jit(solution)/shard_map/pallas_call | solution.py:418
  241.8 12.5 %shard_map.131 = (bf16[1024,8192]{1,0:T(8,128)(2,1)}, bf16[1024,128]{1,0:T(8,128)(2,1)}, bf16[1024,128]{1,0:T(8,128)(2,1)}) custom-call(bf16[1024,8192]{1,0:T(8,128)(2,1)} %get-tuple-element.9.y_in, bf16[1024,128]{1,0:T(8,128)(2,1)} %get-tuple-element.10.k_in, bf16[1024,128]{1,0:T(8,128)(2,1)} %get-tuple-element.11.v_in), custom_call_target="tpu_custom_call" | custom-call | tf_op jit(solution)/shard_map/pallas_call | solution.py:453

commit v3 on v2

--- a/solution.py
+++ b/solution.py
@@ -15,7 +15,7 @@
 ROW_BLOCKS = 4
 K_STEPS = 16
 N_STEPS = 8
-SUBS = 4
+SUBS = 2
 MESH = pl.DeviceIdType.MESH
 
 
@@ -32,7 +32,7 @@
 
 def layer_kernel(cfg, x_hbm, g_ref, cos_ref, sin_ref, wq_hbm, wk_hbm, wv_hbm, wo_hbm, wg_hbm, wu_hbm, wd_hbm,
                  y_hbm, k_hbm, v_hbm,
-                 xbuf, a_buf, wgu, wqkv, wo_buf, wd_buf, acc_gu, acc_qkv, m_buf, o_buf, k_buf, v_buf,
+                 g_row, xbuf, a_buf, wgu, wqkv, wo_buf, wd_buf, acc_gu, acc_qkv, m_buf, o_buf, k_buf, v_buf,
                  pbuf, precv, rsbuf, ybuf, xown,
                  x_sem, wk_sem, wn_sem, kv_sem, xown_sem, ps_send, ps_recv, rs_send, rs_recv, ag_send, ag_recv,
                  yl_sem, yp_send, yp_recv, credit):
@@ -46,6 +46,7 @@
     c_w = half // (2 * ring)
     per_n = n_w // c_w
     s_rows = rows // SUBS
+    stride = (K_STEPS + q_cols // HEAD_DIM + N_STEPS) // (SUBS * (ring - 1))
     q_local = q_cols // HEAD_DIM
     scale = 1.0 / math.sqrt(HEAD_DIM)
     f32, bf16 = jnp.float32, jnp.bfloat16
@@ -197,7 +198,16 @@
             def _():
                 put_out(b, d, k)
 
-    def comm(t, j):
+    def comm(t, step):
+        if isinstance(step, int):
+            if step % stride == 0:
+                comm_piece(t, step // stride)
+        else:
+            @pl.when(lax.rem(step, stride) == 0)
+            def _():
+                comm_piece(t, step // stride)
+
+    def comm_piece(t, j):
         s, sub = j // SUBS, lax.rem(j, SUBS)
 
         @pl.when((s == 0) & (t >= 3))
@@ -220,7 +230,7 @@
         r = pl.ds(pl.multiple_of(i * 16, 16), 16)
         x32 = xbuf[r].astype(f32)
         inv = lax.rsqrt(jnp.mean(x32 * x32, axis=-1, keepdims=True) + NORM_EPS)
-        a_buf[r] = (x32 * inv * g_ref[...].astype(f32)).astype(bf16)
+        a_buf[r] = (x32 * inv * g_row[...]).astype(bf16)
         return carry
 
     def k_step(t, k):
@@ -303,6 +313,9 @@
             ps_copy(t, piece).start()
 
     x_copy(0).start()
+    gains = g_ref[...].astype(f32)
+    for i in range(width // HEAD_DIM):
+        g_row[:, i * HEAD_DIM:(i + 1) * HEAD_DIM] = gains[i:i + 1]
     wgu[:, ff:fpad] = jnp.zeros((3, fpad - ff, k_w), bf16)
     wgu[:, fpad + ff:] = jnp.zeros((3, fpad - ff, k_w), bf16)
     wd_buf[:, ff:] = jnp.zeros((3, fpad - ff, n_w), bf16)
@@ -408,7 +421,7 @@
         c_w = width // (4 * ring)
         s_rows = rows // SUBS
         assert rows % (16 * N_STEPS) == 0
-        assert K_STEPS + q_cols // HEAD_DIM + N_STEPS == SUBS * (ring - 1)
+        assert (K_STEPS + q_cols // HEAD_DIM + N_STEPS) % (SUBS * (ring - 1)) == 0
         cos_full, sin_full = (jnp.asarray(table) for table in rope_tables(tokens))
         cfg = (tokens, width, ff, fpad, q_cols, kv_heads, tp_size)
         bf16, f32 = jnp.bfloat16, jnp.float32
@@ -423,6 +436,7 @@
             in_specs=[any_spec, vmem_spec, vmem_spec, vmem_spec] + [any_spec] * 7,
             out_specs=(any_spec,) * 3,
             scratch_shapes=[
+                vmem((1, width), f32),
                 vmem((rows, width), bf16),
                 vmem((rows, width), bf16),
                 vmem((3, 2 * fpad, k_w), bf16),
@@ -447,7 +461,7 @@
                 pltpu.SemaphoreType.REGULAR,
             ],
             compiler_params=pltpu.CompilerParams(collective_id=0, has_side_effects=True, vmem_limit_bytes=67043328),
-        )(x_in, g_norm.reshape(1, width), cos_full, sin_full, w_q, w_k, w_v, w_o, w_gate.T, w_up.T, w_down)
+        )(x_in, g_norm.reshape(width // HEAD_DIM, HEAD_DIM), cos_full, sin_full, w_q, w_k, w_v, w_o, w_gate.T, w_up.T, w_down)
         pieces = 32
         shapes = (y_out, k_out, v_out)
         y_out, k_out, v_out = pl.pallas_call(

time: 255 us -> 252 us (0.988)
  no operation moved by 1% of the time
where the time goes in v3:
time: 252 us; the launch traced here: 251 us
  Pallas kernels  251 us (100%)
    pallas_call x1, Pallas kernels, local_layer(): pl.pallas_call(functools.partial(layer_kernel, cfg), out_shape=(jax.Shape...  238 us
    pallas_call x1, Pallas kernels, local_layer(): pl.pallas_call(functools.partial(copy_kernel, pieces), out_shape=tuple((j...  12.5 us

profile of v3, /device:TPU:21, one launch (start us, length us, event | category | flops | bytes accessed | tf_op | source)
XLA Modules:
  0.0 251.4 jit_solution(11153320203635068371)
XLA Ops:
  0.6 238.2 %shard_map.130 = (bf16[1024,8192]{1,0:T(8,128)(2,1)}, bf16[1024,128]{1,0:T(8,128)(2,1)}, bf16[1024,128]{1,0:T(8,128)(2,1)}) custom-call(bf16[1024,8192]{1,0:T(8,128)(2,1)} %x_hbm.1, bf16[64,128]{1,0:T(8,128)(2,1)} %bitcast.7, f32[1024,128]{1,0:T(8,128)} %constant.4.clone.cos_ref, f32[1024,128]{1,0:T(8,128)} %constant.5.clone.sin_ref, ...), custom_call_target="tpu_custom_call" | custom-call | tf_op jit(solution)/shard_map/pallas_call | solution.py:431
  238.9 12.5 %shard_map.131 = (bf16[1024,8192]{1,0:T(8,128)(2,1)}, bf16[1024,128]{1,0:T(8,128)(2,1)}, bf16[1024,128]{1,0:T(8,128)(2,1)}) custom-call(bf16[1024,8192]{1,0:T(8,128)(2,1)} %get-tuple-element.9.y_in, bf16[1024,128]{1,0:T(8,128)(2,1)} %get-tuple-element.10.k_in, bf16[1024,128]{1,0:T(8,128)(2,1)} %get-tuple-element.11.v_in), custom_call_target="tpu_custom_call" | custom-call | tf_op jit(solution)/shard_map/pallas_call | solution.py:467
